TPU v7x, 32 devices: a whole 2x2x4 slice. The times are simulated.
32 devices in a mesh: groups: 2 (over x), expert: 8 (over z, y), sub: 2 (over core).
Axes of the slice: x: 2, y: 2, z: 4, core: 2. Of those that a mesh axis runs over, the one named last changes fastest.
Arguments:
- hidden_state: bfloat16 [2048, 2048], P(('groups', 'expert', 'sub')), parts along dimension 0, may hold values from -6 to 6
- norm_gain: float32 [2048], replicated, may hold values from 0.5 to 1.5
- router_weight: bfloat16 [2048, 16], replicated, may hold values from -0.25 to 0.25
- expert_ids: int32 [2048, 6], P(('groups', 'expert', 'sub')), parts along dimension 0, may hold values from 0 to 15, all different within a row; in each aligned block of 64 rows (0 to 63, 64 to 127, ...) at most 32 rows name the same one
- live_counts: int32 [32], P(('groups', 'expert', 'sub')), parts along dimension 0, may hold values from 16 to 64
- routed_gate_up: bfloat16 [16, 2048, 2816], P(('expert', 'sub')), may hold values from -0.125 to 0.125
- routed_down: bfloat16 [16, 1408, 2048], P(('expert', 'sub')), may hold values from -0.15625 to 0.15625
- shared_weights: bfloat16 [3, 2048, 2816], P(None, None, 'expert'), may hold values from -0.125 to 0.125
Outputs:
- mixed: bfloat16 [2048, 2048], P(('groups', 'expert', 'sub')), parts along dimension 0
- penalty: float32 [2], P('groups'), parts along dimension 0
There are 2 independent parts, one for each index of `groups`. A program takes and returns all parts, laid end to end along the dimension named above; an argument that names none is the same for every part. Nothing has to cross between parts.
Inputs may be any that keep to these rules, and one draw needn't show every extreme that they name: `expert_ids`: in each row the 6 experts differ; among the 64 rows of one device no expert is named more than 32 times.
All inputs are finite; a program needn't handle non-finite values.
Results may differ from a plain program's by a relative error of at most 0.0065.
Values may be sent and summed in bfloat16 or wider, within the bound.
A program may use at most 128 MiB of HBM per device.

v0:
```python
import jax
import jax.numpy as jnp
from jax import lax
from jax.sharding import PartitionSpec as P


def normalize(states, norm_gain):
    values = states.astype(jnp.float32)
    spread = jnp.mean(values * values, axis=-1, keepdims=True)
    return (values * lax.rsqrt(spread + 1e-06) * norm_gain).astype(jnp.bfloat16)


def on_device(
    hidden_state,
    norm_gain,
    router_weight,
    expert_ids,
    live_counts,
    routed_gate_up,
    routed_down,
    shared_weights,
):
    tok_rows, width = hidden_state.shape
    choose = expert_ids.shape[1]
    local_experts = routed_gate_up.shape[0]
    hidden_units = routed_down.shape[1]
    expert_count = lax.axis_size("expert")
    sub_count = lax.axis_size("sub")
    devices = expert_count * sub_count
    all_experts = local_experts * devices
    all_tokens = tok_rows * devices
    capacity = (tok_rows * choose * 4 + 3 * all_experts - 1) // (3 * all_experts)
    normed = normalize(hidden_state, norm_gain)
    probs = jax.nn.sigmoid(jnp.dot(normed, router_weight, preferred_element_type=jnp.float32))
    live = (jnp.arange(tok_rows, dtype=jnp.int32) < live_counts[0]).astype(jnp.float32)
    columns = jnp.arange(all_experts, dtype=jnp.int32)
    onehot = (expert_ids[:, :, None] == columns[None, None, :]).astype(jnp.int32)
    picked = jnp.sum(onehot.astype(jnp.float32) * probs[:, None, :], axis=-1)
    weights = (live[:, None] * picked / jnp.sum(picked, axis=-1, keepdims=True)).astype(
        jnp.bfloat16
    )
    live_hot = onehot * live.astype(jnp.int32)[:, None, None]
    flat_hot = live_hot.reshape(tok_rows * choose, all_experts)
    ranks = jnp.cumsum(flat_hot, axis=0) - flat_hot
    slot = jnp.sum(ranks * flat_hot, axis=-1).reshape(tok_rows, choose)
    places = expert_ids * capacity + slot
    cells = jnp.arange(all_experts * capacity, dtype=jnp.int32)
    match = (places[..., None] == cells[None, None, :]).astype(jnp.float32)
    table = (jnp.sum(match, axis=1) * live[:, None]).astype(jnp.bfloat16)
    mixing = jnp.sum(match * weights[:, :, None].astype(jnp.float32), axis=1).astype(jnp.bfloat16)
    send_rows = lax.dot_general(
        table, normed, (((0,), (0,)), ((), ())), preferred_element_type=jnp.float32
    ).astype(jnp.bfloat16)
    load = jnp.sum(flat_hot.astype(jnp.float32), axis=0)
    mass = jnp.sum(probs * live[:, None], axis=0)
    load, mass = lax.psum((load, mass), ("expert", "sub"))
    penalty = all_experts * jnp.sum(load * mass) / (choose * float(all_tokens) * float(all_tokens))
    outgoing = send_rows.reshape(expert_count, sub_count, local_experts, 1, 1, capacity, width)
    arrived = lax.all_to_all(
        lax.all_to_all(outgoing, "expert", split_axis=0, concat_axis=3, tiled=True),
        "sub",
        split_axis=1,
        concat_axis=4,
        tiled=True,
    )
    arrived = arrived.reshape(local_experts, devices * capacity, width)
    inner = jnp.einsum("erd,edf->erf", arrived, routed_gate_up, preferred_element_type=jnp.float32)
    active = (jax.nn.silu(inner[..., :hidden_units]) * inner[..., hidden_units:]).astype(
        jnp.bfloat16
    )
    results = jnp.einsum(
        "erf,efd->erd", active, routed_down, preferred_element_type=jnp.float32
    ).astype(jnp.bfloat16)
    leaving = results.reshape(1, 1, local_experts, expert_count, sub_count, capacity, width)
    returned = lax.all_to_all(
        lax.all_to_all(leaving, "expert", split_axis=3, concat_axis=0, tiled=True),
        "sub",
        split_axis=4,
        concat_axis=1,
        tiled=True,
    )
    returned = returned.reshape(all_experts * capacity, width)
    routed = jnp.dot(mixing, returned, preferred_element_type=jnp.float32)
    piece = lax.all_gather(normed, "expert", axis=0, tiled=True)
    gate_part = jnp.dot(piece, shared_weights[0], preferred_element_type=jnp.float32)
    up_part = jnp.dot(piece, shared_weights[1], preferred_element_type=jnp.float32)
    shared_active = (jax.nn.silu(gate_part) * up_part).astype(jnp.bfloat16)
    partials = lax.dot_general(
        shared_active,
        shared_weights[2],
        (((1,), (1,)), ((), ())),
        preferred_element_type=jnp.float32,
    )
    shared_out = lax.psum_scatter(partials, "expert", scatter_dimension=0, tiled=True)
    mixed = (shared_out + routed).astype(jnp.bfloat16)
    return (mixed, penalty.reshape(1))


def solution(mesh):
    placed = (
        P(("groups", "expert", "sub"), None),
        P(),
        P(),
        P(("groups", "expert", "sub"), None),
        P(("groups", "expert", "sub")),
        P(("expert", "sub"), None, None),
        P(("expert", "sub"), None, None),
        P(None, None, "expert"),
    )
    return jax.shard_map(
        on_device,
        mesh=mesh,
        in_specs=placed,
        out_specs=(P(("groups", "expert", "sub"), None), P("groups")),
        check_vma=False,
    )
```

profile of v0, /device:TPU:0, one launch (start us, length us, event | category | flops | bytes accessed | tf_op | source)
XLA Modules:
  0.0 230.8 jit_solution(11255642411621888006)
XLA Ops:
  7.2 0.0 copy-start
  7.2 0.0 all-gather.2.cloned.1.call-start
  7.2 1.1 fusion.39
  8.3 1.8 fusion.41
  10.1 0.0 all-gather.2.cloned.1.call-update
  10.8 0.1 mul.116
  10.9 0.1 mul.120
  11.0 0.1 mul.117
  11.2 0.8 copy.56
  12.0 0.1 eq.49
  12.1 0.1 eq.45
  12.3 0.9 reduce-window.6
  13.1 0.2 slice_reduce_fusion
  13.4 0.1 fusion.47
  13.5 0.1 reshape.129
  13.6 0.1 copy.59
  13.7 0.0 copy-done
  13.7 1.3 multiply_reduce_fusion
  15.0 0.7 fusion.45
  15.7 0.7 multiply_add_fusion
  16.4 0.2 select_reduce_fusion
  16.6 3.1 %convolution_convert_fusion = bf16[512,2048]{1,0:T(8,128)(2,1)} fusion(bf16[64,2048]{1,0:T(8,128)(2,1)} %fusion.41, f32[64,512]{1,0:T(8,128)S(1)} %get-tuple-element.5, f32[64]{0:T(128)S(1)} %get-tuple-element.10), kind=kOutput, calls=%fused_computation.5 | convolution fusion | flops 135331840 | bytes 2490624 | tf_op jit(solution)/shard_map/dot_general | solution.py:51
  19.7 7.3 %all-to-all-start = ((bf16[8,2,1,1,1,32,2048]{6,5,1,4,3,2,0:T(8,128)(2,1)}), bf16[8,2,1,1,1,32,2048]{6,5,1,4,3,2,0:T(8,128)(2,1)S(1)}, u32[]{:S(2)}, u32[]{:S(2)}) async-start(bf16[8,2,1,1,1,32,2048]{6,5,1,4,3,2,0:T(8,128)(2,1)} %bitcast.73), calls=%async_computation.1 | async-start | bytes 4194304 | tf_op jit(solution)/shard_map/all_to_all | solution.py:60
  27.0 0.0 reduce-scatter.2.cloned.1.call-start
  27.0 67.8 %all-gather.2.cloned.1.call-done = bf16[512,2048]{1,0:T(8,128)(2,1)} async-done(((bf16[64,2048]{1,0:T(8,128)(2,1)}), bf16[512,2048]{1,0:T(8,128)(2,1)}) %all-gather.2.cloned.1.call-update) | async-done | bytes 2097168 | tf_op jit(solution)/shard_map/all_gather | solution.py:84
  94.8 2.9 %fusion.17 = f32[512,352]{0,1:T(8,128)S(1)} fusion(bf16[512,2048]{1,0:T(8,128)(2,1)} %all-gather.2.cloned.1.call-done, bf16[3,2048,352]{1,2,0:T(8,128)(2,1)} %param.15), kind=kOutput, calls=%fused_computation.16 | convolution fusion | flops 738197504 | bytes 4259840 | tf_op jit(solution)/shard_map/dot_general | solution.py:85
  97.8 6.6 %fusion.13 = f32[512,2048]{1,0:T(8,128)} fusion(bf16[3,2048,352]{1,2,0:T(8,128)(2,1)} %param.15, bf16[512,2048]{1,0:T(8,128)(2,1)} %all-gather.2.cloned.1.call-done, f32[512,352]{0,1:T(8,128)S(1)} %fusion.17), kind=kOutput, calls=%fused_computation.12 | convolution fusion | flops 1477476352 | bytes 9895936 | tf_op jit(solution)/shard_map/dot_general | solution.py:88
  104.3 0.0 reduce-scatter.2.cloned.1.call-update
  104.4 0.0 all-to-all-done
  104.4 0.1 copy.61
  104.5 5.4 %all_to_all.54 = bf16[1,2,1,8,1,32,2048]{6,5,3,4,2,0,1:T(8,128)(2,1)S(1)} all-to-all(bf16[1,2,1,8,1,32,2048]{6,5,3,4,2,0,1:T(8,128)(2,1)S(1)} %copy.61), channel_id=1, replica_groups=mesh['groups'=2,'expert'=8,'sub'=2] {'sub'}, dimensions={1} | all-to-all | bytes 4194304 | tf_op jit(solution)/shard_map/all_to_all | solution.py:59
  109.9 0.0 slice-start
  109.9 0.2 copy.62
  110.2 0.0 slice-start.1
  110.2 9.6 %fusion.4 = f32[1,512,2816]{2,1,0:T(8,128)S(1)} fusion(bf16[512,2048]{1,0:T(8,128)(2,1)S(1)} %bitcast.76, bf16[1,2048,2816]{2,1,0:T(8,128)(2,1)} %param.13), kind=kOutput, calls=%fused_computation.4 | convolution fusion | flops 5905580032 | bytes 19398656 | tf_op jit(solution)/shard_map/erd,edf->erf/dot_general | solution.py:67
  119.8 0.0 slice-done
  119.9 0.0 slice-done.1
  119.9 4.7 %fusion.7 = bf16[512,2048]{1,0:T(8,128)(2,1)} fusion(bf16[1,1408,2048]{2,1,0:T(8,128)(2,1)S(1)} %bitcast.79, f32[1,512,2816]{2,1,0:T(8,128)S(1)} %fusion.4), kind=kOutput, calls=%fused_computation.6 | convolution fusion | flops 2958163968 | bytes 13631488 | tf_op jit(solution)/shard_map/erf,efd->erd/dot_general | solution.py:71
  124.6 3.6 %all-to-all-start.2 = ((bf16[1,1,1,8,2,32,2048]{6,5,4,2,1,0,3:T(8,128)(2,1)}), bf16[1,1,1,8,2,32,2048]{6,5,4,2,1,0,3:T(8,128)(2,1)S(1)}, u32[]{:S(2)}, u32[]{:S(2)}) async-start(bf16[1,1,1,8,2,32,2048]{6,5,4,2,1,0,3:T(8,128)(2,1)} %bitcast.75), calls=%async_computation.3 | async-start | bytes 4194304 | tf_op jit(solution)/shard_map/all_to_all | solution.py:76
  128.2 0.1 fusion.48
  128.3 75.5 %all-reduce = (f32[16]{0:T(128)S(1)}, f32[16]{0:T(128)S(1)}) all-reduce(f32[16]{0:T(128)S(1)} %fusion.48, f32[16]{0:T(128)S(1)} %get-tuple-element.8), channel_id=1, replica_groups=mesh['groups'=2,'expert'=8,'sub'=2] {'expert','sub'}, use_global_device_ids=true, to_apply=%region_10.11 | all-reduce | flops 32 | bytes 256 | tf_op jit(solution)/shard_map/psum | solution.py:56
  203.8 0.6 multiply_reduce_fusion.1
  205.0 0.0 all-to-all-done.2
  205.1 0.1 copy.64
  205.2 5.4 %all_to_all.55 = bf16[8,1,1,1,2,32,2048]{6,5,0,3,2,1,4:T(8,128)(2,1)S(1)} all-to-all(bf16[8,1,1,1,2,32,2048]{6,5,0,3,2,1,4:T(8,128)(2,1)S(1)} %copy.64), channel_id=1, replica_groups=mesh['groups'=2,'expert'=8,'sub'=2] {'sub'}, dimensions={4} | all-to-all | bytes 4194304 | tf_op jit(solution)/shard_map/all_to_all | solution.py:75
  210.6 0.1 copy.65
  210.8 9.8 %reduce-scatter.2.cloned.1.call-done = f32[64,2048]{1,0:T(8,128)} async-done(((f32[512,2048]{1,0:T(8,128)}), f32[64,2048]{1,0:T(8,128)}) %reduce-scatter.2.cloned.1.call-update) | async-done | bytes 524304 | tf_op jit(solution)/shard_map/reduce_scatter | solution.py:94
  220.5 2.2 fusion.11
  (6 shorter events, 0.1 us)
Async XLA Ops:
  7.2 6.5 %copy-start = (bf16[2048,16]{0,1:T(8,128)(2,1)S(1)}, bf16[2048,16]{0,1:T(8,128)(2,1)}, u32[]{:S(2)}) copy-start(bf16[2048,16]{0,1:T(8,128)(2,1)} %param.10) | copy-start | bytes 196612
  7.2 87.6 %all-gather.2.cloned.1.call-start = ((), (), s32[]{:S(2)}) async-start(), calls=%async_computation.5 | async-start | bytes 2359296 | tf_op jit(solution)/shard_map/all_gather | solution.py:84
  19.7 84.7 %all-to-all-start = ((bf16[8,2,1,1,1,32,2048]{6,5,1,4,3,2,0:T(8,128)(2,1)}), bf16[8,2,1,1,1,32,2048]{6,5,1,4,3,2,0:T(8,128)(2,1)S(1)}, u32[]{:S(2)}, u32[]{:S(2)}) async-start(bf16[8,2,1,1,1,32,2048]{6,5,1,4,3,2,0:T(8,128)(2,1)} %bitcast.73), calls=%async_computation.1 | async-start | bytes 4194304 | tf_op jit(solution)/shard_map/all_to_all | solution.py:60
  27.0 193.5 %reduce-scatter.2.cloned.1.call-start = ((), (), s32[]{:S(2)}) async-start(), calls=%async_computation.6 | async-start | bytes 4718592 | tf_op jit(solution)/shard_map/reduce_scatter | solution.py:94
  109.9 9.9 %slice-start = ((s8[5767168]{0:T(1024)(128)(4,1)}), s8[4194304]{0:T(1024)(128)(4,1)S(1)}, s32[]{:S(2)}) async-start(s8[5767168]{0:T(1024)(128)(4,1)} %bitcast.78), calls=%async_computation.7 | async-start | bytes 8388608
  110.2 9.7 %slice-start.1 = ((s8[5767168]{0:T(1024)(128)(4,1)}), s8[1572864]{0:T(1024)(128)(4,1)S(1)}, s32[]{:S(2)}) async-start(s8[5767168]{0:T(1024)(128)(4,1)} %bitcast.78), calls=%async_computation.8 | async-start | bytes 3145728
  124.6 80.5 %all-to-all-start.2 = ((bf16[1,1,1,8,2,32,2048]{6,5,4,2,1,0,3:T(8,128)(2,1)}), bf16[1,1,1,8,2,32,2048]{6,5,4,2,1,0,3:T(8,128)(2,1)S(1)}, u32[]{:S(2)}, u32[]{:S(2)}) async-start(bf16[1,1,1,8,2,32,2048]{6,5,4,2,1,0,3:T(8,128)(2,1)} %bitcast.75), calls=%async_computation.3 | async-start | bytes 4194304 | tf_op jit(solution)/shard_map/all_to_all | solution.py:76
Sparse Core Ops, SparseCore 0:
  10.7 84.0 all-gather.1
  104.5 116.0 reduce-scatter.1
where the time goes:
time: 231 us
  blocking collectives  86.3 us (37%)
  waiting for transfers between devices  77.6 us (34%)
  matrix products  30.4 us (13%)
  between operations  16.6 us (7%)
  starting transfers between devices  11 us (5%)
  other arithmetic  6.26 us (3%)
  local copies, waits for them, and re-layouts  2.5 us (1%)
    psum x1, blocking collectives, on_device(): load, mass = lax.psum((load, mass), ('expert', 'sub'))  75.5 us
    all_gather x1, waiting for transfers between devices, on_device(): piece = lax.all_gather(normed, 'expert', axis=0, tiled=True)  67.8 us
    reduce_scatter x1, waiting for transfers between devices, on_device(): lax.psum_scatter(partials, 'expert', scatter_dimension=0, tiled=True)  9.78 us
    dot_general x1, matrix products, on_device(): jnp.einsum('erd,edf->erf', arrived, routed_gate_up, preferred_element_typ...  9.64 us
    all_to_all x1, starting transfers between devices, on_device(): lax.all_to_all(outgoing, 'expert', split_axis=0, concat_axis=3, tiled=True)  7.31 us
    dot_general x1, matrix products, on_device(): lax.dot_general(shared_active, shared_weights[2], (((1,), (1,)), ((), ())...  6.58 us
    all_to_all x1, blocking collectives, on_device(): lax.all_to_all(lax.all_to_all(outgoing, 'expert', split_axis=0, concat_ax...  5.42 us
    all_to_all x1, blocking collectives, on_device(): lax.all_to_all(lax.all_to_all(leaving, 'expert', split_axis=3, concat_axi...  5.42 us
  transfers between devices with their start and end apart: 4, of which 2 were waited for; matrix products, arithmetic and copies ran while one was open for 15% of the time, Pallas kernels for 0%

commit v1 on v0

v1 whole, which is shorter than its diff:
```python
import jax
import jax.numpy as jnp
from jax import lax
from jax.sharding import PartitionSpec as P

BOTH = ("expert", "sub")


def normalize(states, norm_gain):
    values = states.astype(jnp.float32)
    spread = jnp.mean(values * values, axis=-1, keepdims=True)
    return (values * lax.rsqrt(spread + 1e-06) * norm_gain).astype(jnp.bfloat16)


def on_device(
    hidden_state,
    norm_gain,
    router_weight,
    expert_ids,
    live_counts,
    routed_gate_up,
    routed_down,
    shared_weights,
):
    tok_rows, width = hidden_state.shape
    choose = expert_ids.shape[1]
    local_experts = routed_gate_up.shape[0]
    hidden_units = routed_down.shape[1]
    chips = lax.axis_size("expert")
    subs = lax.axis_size("sub")
    devices = chips * subs
    all_experts = local_experts * devices
    all_tokens = tok_rows * devices
    capacity = (tok_rows * choose * 4 + 3 * all_experts - 1) // (3 * all_experts)
    my_sub = lax.axis_index("sub")
    me = lax.axis_index("expert") * subs + my_sub

    normed = normalize(hidden_state, norm_gain)
    everyone = lax.all_gather(normed, BOTH, axis=0, tiled=True)
    probs = jax.nn.sigmoid(jnp.dot(normed, router_weight, preferred_element_type=jnp.float32))
    live = (jnp.arange(tok_rows, dtype=jnp.int32) < live_counts[0]).astype(jnp.float32)
    columns = jnp.arange(all_experts, dtype=jnp.int32)
    hot = jnp.sum((expert_ids[:, :, None] == columns[None, None, :]).astype(jnp.float32), axis=1)
    picked = hot * probs
    weights = live[:, None] * picked / jnp.sum(picked, axis=-1, keepdims=True)
    live_hot = hot * live[:, None]
    notes = jnp.concatenate([weights, live_hot, probs * live[:, None]], axis=-1)
    notes = lax.all_gather(notes, BOTH, axis=0, tiled=True)
    load = jnp.sum(notes[:, all_experts : 2 * all_experts], axis=0)
    mass = jnp.sum(notes[:, 2 * all_experts :], axis=0)
    penalty = all_experts * jnp.sum(load * mass) / (choose * float(all_tokens) * float(all_tokens))

    owner = jnp.arange(all_tokens, dtype=jnp.int32) // tok_rows
    cells = jnp.arange(devices * capacity, dtype=jnp.int32)
    mixed = None
    for item in range(local_experts):
        column = me * local_experts + item
        chosen = lax.dynamic_slice_in_dim(notes, all_experts + column, 1, axis=1)
        weight = lax.dynamic_slice_in_dim(notes, column, 1, axis=1).astype(jnp.bfloat16)
        by_owner = chosen.reshape(devices, tok_rows)
        before = jnp.arange(tok_rows)[:, None] < jnp.arange(tok_rows)[None, :]
        rank = jnp.dot(by_owner, before.astype(jnp.float32)).reshape(all_tokens)
        place = jnp.where(chosen[:, 0] > 0, rank.astype(jnp.int32) + owner * capacity, -1)
        match = place[:, None] == cells[None, :]
        table = match.astype(jnp.bfloat16)
        rows = lax.dot_general(
            table, everyone, (((0,), (0,)), ((), ())), preferred_element_type=jnp.float32
        ).astype(jnp.bfloat16)
        inner = jnp.dot(rows, routed_gate_up[item], preferred_element_type=jnp.float32)
        active = (jax.nn.silu(inner[:, :hidden_units]) * inner[:, hidden_units:]).astype(
            jnp.bfloat16
        )
        results = jnp.dot(active, routed_down[item], preferred_element_type=jnp.float32).astype(
            jnp.bfloat16
        )
        mixing = jnp.where(match, weight, jnp.zeros((), jnp.bfloat16))
        part = jnp.dot(mixing, results, preferred_element_type=jnp.float32)
        mixed = part if mixed is None else mixed + part

    piece = lax.dynamic_index_in_dim(
        everyone.reshape(chips, subs, tok_rows, width), my_sub, axis=1, keepdims=False
    ).reshape(chips * tok_rows, width)
    gate_part = jnp.dot(piece, shared_weights[0], preferred_element_type=jnp.float32)
    up_part = jnp.dot(piece, shared_weights[1], preferred_element_type=jnp.float32)
    shared_active = (jax.nn.silu(gate_part) * up_part).astype(jnp.bfloat16)
    partials = lax.dot_general(
        shared_active,
        shared_weights[2],
        (((1,), (1,)), ((), ())),
        preferred_element_type=jnp.float32,
    )
    mine = (jnp.arange(subs) == my_sub)[None, :, None, None]
    partials = jnp.where(mine, partials.reshape(chips, 1, tok_rows, width), 0.0)
    total = (mixed.reshape(chips, subs, tok_rows, width) + partials).astype(jnp.bfloat16)
    total = total.reshape(all_tokens, width)
    mixed = lax.psum_scatter(total, BOTH, scatter_dimension=0, tiled=True)
    return (mixed.astype(jnp.bfloat16), penalty.reshape(1))


def solution(mesh):
    placed = (
        P(("groups", "expert", "sub"), None),
        P(),
        P(),
        P(("groups", "expert", "sub"), None),
        P(("groups", "expert", "sub")),
        P(("expert", "sub"), None, None),
        P(("expert", "sub"), None, None),
        P(None, None, "expert"),
    )
    return jax.shard_map(
        on_device,
        mesh=mesh,
        in_specs=placed,
        out_specs=(P(("groups", "expert", "sub"), None), P("groups")),
        check_vma=False,
    )
```

time: 231 us -> 186 us (0.81)
  blocking collectives: 86.3 us -> 25.2 us
  waiting for transfers between devices: 77.6 us -> 96.1 us
  starting transfers between devices: 11 us -> 0.08 us
  matrix products: 30.4 us -> 40.2 us
    psum x1 -> x0, blocking collectives: 75.5 us -> none  [on_device(): load, mass = lax.psum((load, mass), ('expert', 'sub'))]
    reduce_scatter x1, waiting for transfers between devices: 9.78 us -> 70.1 us  [on_device(): mixed = lax.psum_scatter(total, BOTH, scatter_dimension=0, tiled=True)]
    all_gather x1, waiting for transfers between devices: 67.8 us -> 26 us  [on_device(): everyone = lax.all_gather(normed, BOTH, axis=0, tiled=True)]
    all_gather x0 -> x1, blocking collectives: none -> 25.2 us  [on_device(): notes = lax.all_gather(notes, BOTH, axis=0, tiled=True)]
    dot_general x4 -> x5, matrix products: 19.6 us -> 32.1 us  [the longest x1 17 us: on_device(): jnp.dot(rows, routed_gate_up[item], preferred_element_type=jnp.float32)]
    all_to_all x2 -> x0, starting transfers between devices: 10.9 us -> none  [the longest x1 7.31 us: on_device(): lax.all_to_all(outgoing, 'expert', split_axis=0, concat_axis=3, tiled=True)]
    all_to_all x2 -> x0, blocking collectives: 10.8 us -> none  [the longest x1 5.42 us: on_device(): lax.all_to_all(lax.all_to_all(outgoing, 'expert', split_axis=0, concat_ax...]
  transfers between devices with their start and end apart: 4 -> 2, of which waited for: 2 -> 2; matrix products, arithmetic and copies ran while one was open for 15% -> 2% of each run, Pallas kernels for 0% -> 0%
where the time goes in v1:
time: 186 us; the launch traced here: 185 us
  waiting for transfers between devices  96.1 us (52%)
  matrix products  40.2 us (22%)
  blocking collectives  25.2 us (14%)
  between operations  16.6 us (9%)
  other arithmetic  4.37 us (2%)
  local copies, waits for them, and re-layouts  2.62 us (1%)
    reduce_scatter x1, waiting for transfers between devices, on_device(): mixed = lax.psum_scatter(total, BOTH, scatter_dimension=0, tiled=True)  70.1 us
    all_gather x1, waiting for transfers between devices, on_device(): everyone = lax.all_gather(normed, BOTH, axis=0, tiled=True)  26 us
    all_gather x1, blocking collectives, on_device(): notes = lax.all_gather(notes, BOTH, axis=0, tiled=True)  25.2 us
    dot_general x1, matrix products, on_device(): jnp.dot(rows, routed_gate_up[item], preferred_element_type=jnp.float32)  17 us
    dot_general x1, matrix products, on_device(): jnp.dot(active, routed_down[item], preferred_element_type=jnp.float32)  8.11 us
    dot_general x1, matrix products, on_device(): lax.dot_general(shared_active, shared_weights[2], (((1,), (1,)), ((), ())...  4.65 us
    dot_general x1, matrix products, on_device(): part = jnp.dot(mixing, results, preferred_element_type=jnp.float32)  4.48 us
  transfers between devices with their start and end apart: 2, of which 2 were waited for; matrix products, arithmetic and copies ran while one was open for 2% of the time, Pallas kernels for 0%

profile of v1, /device:TPU:0, one launch (start us, length us, event | category | flops | bytes accessed | tf_op | source)
XLA Modules:
  0.0 185.2 jit_solution(10021006158538988017)
XLA Ops:
  7.2 0.0 copy-start
  7.2 0.0 all-gather.3.cloned.1.call-start
  7.2 1.1 fusion.34
  8.3 1.8 fusion.36
  10.1 0.0 all-gather.3.cloned.1.call-update
  10.2 0.0 reduce-scatter.2.cloned.1.call-start
  10.9 0.7 convert_reduce_fusion
  11.6 0.0 copy-done
  11.6 1.2 multiply_reduce_fusion
  12.8 25.2 %all-gather = f32[16,64,48]{1,2,0:T(8,128)S(1)} all-gather(f32[1,64,48]{1,2,0:T(8,128)S(1)} %maximum_bitcast_fusion), channel_id=1, replica_groups=mesh['groups'=2,'expert'=8,'sub'=2] {'expert','sub'}, dimensions={0}, use_global_device_ids=true | all-gather | bytes 208896 | tf_op jit(solution)/shard_map/all_gather | solution.py:48
  38.0 0.1 copy.18
  38.1 0.2 reshape.107
  38.3 0.1 reshape.101
  38.4 0.1 convolution_convert_fusion.1
  38.5 0.1 convert_element_type.55
  38.6 0.1 broadcast_in_dim.58
  38.7 0.1 broadcast_in_dim.59
  38.8 26.0 %all-gather.3.cloned.1.call-done = bf16[1024,2048]{1,0:T(8,128)(2,1)} async-done(((bf16[64,2048]{1,0:T(8,128)(2,1)}), bf16[1024,2048]{1,0:T(8,128)(2,1)}) %all-gather.3.cloned.1.call-update) | async-done | bytes 4194320 | tf_op jit(solution)/shard_map/all_gather | solution.py:39
  64.8 1.7 constant_dynamic-slice_fusion
  66.5 2.3 %fusion.16 = f32[512,352]{0,1:T(8,128)S(1)} fusion(bf16[512,2048]{1,0:T(8,128)(2,1)S(1)} %bitcast.47, bf16[3,2048,352]{1,2,0:T(8,128)(2,1)} %param.15), kind=kOutput, calls=%fused_computation.17 | convolution fusion | flops 738197504 | bytes 4259840 | tf_op jit(solution)/shard_map/dot_general | solution.py:83
  68.9 2.4 %fusion.25 = bf16[512,352]{0,1:T(8,128)(2,1)S(1)} fusion(bf16[512,2048]{1,0:T(8,128)(2,1)S(1)} %bitcast.48, bf16[3,2048,352]{1,2,0:T(8,128)(2,1)} %param.15, f32[512,352]{0,1:T(8,128)S(1)} %fusion.16), kind=kOutput, calls=%fused_computation.24 | convolution fusion | flops 739278848 | bytes 4620288 | tf_op jit(solution)/shard_map/dot_general | solution.py:84
  71.2 0.2 copy.19
  71.5 4.6 %fusion.12 = f32[8,64,2048]{2,1,0:T(8,128)} fusion(bf16[8,64,352]{2,1,0:T(8,128)(2,1)S(1)} %bitcast.49, bf16[3,2048,352]{1,2,0:T(8,128)(2,1)} %param.15), kind=kOutput, calls=%fused_computation.13 | convolution fusion | flops 738197504 | bytes 5996544 | tf_op jit(solution)/shard_map/dot_general | solution.py:86
  76.1 17.0 %fusion = f32[512,2816]{1,0:T(8,128)} fusion(bf16[1,2048,2816]{2,1,0:T(8,128)(2,1)} %param.13, bf16[1024,2048]{1,0:T(8,128)(2,1)} %all-gather.3.cloned.1.call-done, s32[1024]{0:T(1024)S(1)} %bitcast.51), kind=kOutput, calls=%fused_computation | convolution fusion | flops 8054636544 | bytes 21499904 | tf_op jit(solution)/shard_map/dot_general | solution.py:69
  93.1 0.0 copy-start.1
  93.1 8.1 %fusion.6 = bf16[512,2048]{1,0:T(8,128)(2,1)S(1)} fusion(bf16[1,1408,2048]{2,1,0:T(8,128)(2,1)} %param.14, f32[512,2816]{1,0:T(8,128)} %fusion), kind=kOutput, calls=%fused_computation.8 | convolution fusion | flops 2958163968 | bytes 13631488 | tf_op jit(solution)/shard_map/dot_general | solution.py:73
  101.2 0.0 copy-done.1
  101.2 4.5 %fusion.3 = bf16[1024,2048]{1,0:T(8,128)(2,1)} fusion(f32[8,64,2048]{2,1,0:T(8,128)S(1)} %copy-done.1, pred[1024]{0:T(1024)(128)(4,1)S(1)} %broadcast_in_dim.59, bf16[512,2048]{1,0:T(8,128)(2,1)S(1)} %fusion.6, s32[1024]{0:T(1024)S(1)} %bitcast.52, bf16[1024]{0:T(1024)(128)(2,1)S(1)} %convert_reduce_fusion.1), kind=kOutput, calls=%fused_computation.4 | convolution fusion | flops 2154823680 | bytes 10492928 | tf_op jit(solution)/shard_map/dot_general | solution.py:77
  105.7 0.0 reduce-scatter.2.cloned.1.call-update
  105.7 0.1 slice_reduce_fusion
  105.8 0.6 multiply_reduce_fusion.1
  107.1 70.1 %reduce-scatter.2.cloned.1.call-done = bf16[64,2048]{1,0:T(8,128)(2,1)} async-done(((bf16[1024,2048]{1,0:T(8,128)(2,1)}), bf16[64,2048]{1,0:T(8,128)(2,1)}) %reduce-scatter.2.cloned.1.call-update) | async-done | bytes 262160 | tf_op jit(solution)/shard_map/reduce_scatter | solution.py:96
  (8 shorter events, 0.1 us)
Async XLA Ops:
  7.2 4.4 %copy-start = (bf16[2048,16]{0,1:T(8,128)(2,1)S(1)}, bf16[2048,16]{0,1:T(8,128)(2,1)}, u32[]{:S(2)}) copy-start(bf16[2048,16]{0,1:T(8,128)(2,1)} %param.10) | copy-start | bytes 196612
  7.2 57.6 %all-gather.3.cloned.1.call-start = ((), (), s32[]{:S(2)}) async-start(), calls=%async_computation.1 | async-start | bytes 4456448 | tf_op jit(solution)/shard_map/all_gather | solution.py:39
  10.2 167.0 %reduce-scatter.2.cloned.1.call-start = ((), (), s32[]{:S(2)}) async-start(), calls=%async_computation.2 | async-start | bytes 4456448 | tf_op jit(solution)/shard_map/reduce_scatter | solution.py:96
  93.1 8.1 %copy-start.1 = (f32[8,64,2048]{2,1,0:T(8,128)S(1)}, f32[8,64,2048]{2,1,0:T(8,128)}, u32[]{:S(2)}) copy-start(f32[8,64,2048]{2,1,0:T(8,128)} %fusion.12) | copy-start | bytes 12582916
Sparse Core Ops, SparseCore 0:
  10.7 54.0 all-gather.2
  105.8 71.3 reduce-scatter.1

commit v2 on v1

v2 whole, which is shorter than its diff:
```python
import functools

import jax
import jax.numpy as jnp
from jax import lax
from jax.experimental import pallas as pl
from jax.experimental.pallas import tpu as pltpu
from jax.sharding import PartitionSpec as P

MESH = pl.DeviceIdType.MESH


def ring_place(chip, chips, fold):
    if fold == 1:
        return chip
    row, step = chip % 2, chip // 2
    return (1 - row) * step + row * (chips - 1 - step)


def ring_chip(place, chips, fold):
    if fold == 1:
        return place
    back = place // (chips // 2)
    step = (1 - back) * place + back * (chips - 1 - place)
    return 2 * step + back


def neighbours(chips, subs, fold):
    sub = lax.axis_index("sub")
    chip = lax.axis_index("expert")
    place = ring_place(chip, chips, fold)
    right = ring_chip((place + 1) % chips, chips, fold)
    left = ring_chip((place + chips - 1) % chips, chips, fold)
    along = [{"expert": right, "sub": sub}, {"expert": left, "sub": sub}]
    peers = [{"expert": chip, "sub": (sub + i) % subs} for i in range(1, subs)]
    return along, peers


def greet(along, peers):
    barrier = pltpu.get_barrier_semaphore()
    for target in along + peers:
        pl.semaphore_signal(barrier, inc=1, device_id=target, device_id_type=MESH)
    pl.semaphore_wait(barrier, len(along) + len(peers))


def carried(chips, hop, way, pieces):
    if 2 * hop < chips:
        return range(pieces)
    if 2 * hop == chips:
        return [0, 2] if way == 0 else [1]
    return []


def gather_kernel(
    chips, subs, fold, block_ref, notes_ref, all_ref, all_notes_ref,
    ring_send, ring_recv, peer_send, peer_recv, own_sem,
):
    along, peers = neighbours(chips, subs, fold)
    rows = block_ref.shape[0]
    half = rows // 2
    hops = chips // 2

    def piece(r, k, j):
        if j == 2:
            return all_notes_ref.at[r, k % chips]
        return all_ref.at[r, k % chips, pl.ds(j * half, half)]

    def own_piece(j):
        if j == 2:
            return notes_ref
        return block_ref.at[pl.ds(j * half, half)]

    def ring_copy(way, hop, j):
        sign = -1 if way == 0 else 1
        source = own_piece(j) if hop == 1 else piece(0, sign * (hop - 1), j)
        return pltpu.make_async_remote_copy(
            src_ref=source,
            dst_ref=piece(0, sign * hop, j),
            send_sem=ring_send.at[way, hop - 1, j],
            recv_sem=ring_recv.at[way, hop - 1, j],
            device_id=along[way],
            device_id_type=MESH,
        )

    def peer_copy(i, k, j):
        source = own_piece(j) if k == 0 else piece(0, k, j)
        return pltpu.make_async_remote_copy(
            src_ref=source,
            dst_ref=piece(subs - i, k, j),
            send_sem=peer_send.at[i - 1, k % chips, j],
            recv_sem=peer_recv.at[i - 1, k % chips, j],
            device_id=peers[i - 1],
            device_id_type=MESH,
        )

    keep = [
        pltpu.make_async_copy(block_ref, all_ref.at[0, 0], own_sem.at[0]),
        pltpu.make_async_copy(notes_ref, all_notes_ref.at[0, 0], own_sem.at[1]),
    ]
    greet(along, peers)
    started, pending = [], []
    for j in (2, 0, 1):
        for way in range(2):
            if j in carried(chips, 1, way, 3):
                copy = ring_copy(way, 1, j)
                copy.start()
                started.append(copy)
    for j in range(3):
        for i in range(1, subs):
            copy = peer_copy(i, 0, j)
            copy.start()
            started.append(copy)
            pending.append(copy)
    for copy in keep:
        copy.start()
    for hop in range(1, hops + 1):
        for j in (2, 0, 1):
            for way in range(2):
                if j not in carried(chips, hop, way, 3):
                    continue
                ring_copy(way, hop, j).wait_recv()
                if j in carried(chips, hop + 1, way, 3):
                    copy = ring_copy(way, hop + 1, j)
                    copy.start()
                    started.append(copy)
                for i in range(1, subs):
                    copy = peer_copy(i, -hop if way == 0 else hop, j)
                    copy.start()
                    started.append(copy)
                    pending.append(copy)
    for copy in pending:
        copy.wait_recv()
    for copy in started:
        copy.wait_send()
    for copy in keep:
        copy.wait()


def scatter_kernel(
    chips, subs, fold, part_ref, out_ref, from_peer, going, coming,
    ring_send, ring_recv, peer_send, peer_recv,
):
    along, peers = neighbours(chips, subs, fold)
    rows = out_ref.shape[0]
    half = rows // 2
    hops = chips // 2

    def peer_copy(i, k):
        k = k % chips
        return pltpu.make_async_remote_copy(
            src_ref=part_ref.at[i, k],
            dst_ref=from_peer.at[i - 1, k],
            send_sem=peer_send.at[i - 1, k],
            recv_sem=peer_recv.at[i - 1, k],
            device_id=peers[i - 1],
            device_id_type=MESH,
        )

    def ring_copy(way, hop, j):
        spot = (way, hop - 1, pl.ds(j * half, half))
        return pltpu.make_async_remote_copy(
            src_ref=going.at[spot],
            dst_ref=coming.at[spot],
            send_sem=ring_send.at[way, hop - 1, j],
            recv_sem=ring_recv.at[way, hop - 1, j],
            device_id=along[way],
            device_id_type=MESH,
        )

    def local_sum(k, j):
        span = pl.ds(j * half, half)
        value = part_ref[0, k % chips, span, :].astype(jnp.float32)
        for i in range(1, subs):
            value = value + from_peer[i - 1, k % chips, span, :].astype(jnp.float32)
        return value

    greet(along, peers)
    order = []
    for hop in range(hops, 0, -1):
        for k in (hop, -hop):
            if k % chips not in order:
                order.append(k % chips)
    order.append(0)
    sent = []
    for k in order:
        for i in range(1, subs):
            copy = peer_copy(i, k)
            copy.start()
            sent.append(copy)
    here = set()

    def need(k):
        if k % chips not in here:
            here.add(k % chips)
            for i in range(1, subs):
                peer_copy(i, k).wait_recv()

    for hop in range(hops, 0, -1):
        for j in range(2):
            for way in range(2):
                if j not in carried(chips, hop, way, 2):
                    continue
                k = hop if way == 0 else -hop
                need(k)
                value = local_sum(k, j)
                if j in carried(chips, hop + 1, way, 2):
                    ring_copy(way, hop + 1, j).wait_recv()
                    value = value + coming[way, hop, pl.ds(j * half, half), :].astype(jnp.float32)
                going[way, hop - 1, pl.ds(j * half, half), :] = value.astype(going.dtype)
                copy = ring_copy(way, hop, j)
                copy.start()
                sent.append(copy)
    need(0)
    for j in range(2):
        value = local_sum(0, j)
        for way in range(2):
            if j in carried(chips, 1, way, 2):
                ring_copy(way, 1, j).wait_recv()
                value = value + coming[way, 0, pl.ds(j * half, half), :].astype(jnp.float32)
        out_ref[pl.ds(j * half, half), :] = value.astype(out_ref.dtype)
    for copy in sent:
        copy.wait_send()


def ring_gather(block, notes, chips, subs, fold):
    hops = max(chips // 2, 1)
    vmem = pl.BlockSpec(memory_space=pltpu.VMEM)
    return pl.pallas_call(
        functools.partial(gather_kernel, chips, subs, fold),
        out_shape=(
            jax.ShapeDtypeStruct((subs, chips) + block.shape, block.dtype),
            jax.ShapeDtypeStruct((subs, chips) + notes.shape, notes.dtype),
        ),
        in_specs=[vmem, vmem],
        out_specs=(vmem, vmem),
        scratch_shapes=[
            pltpu.SemaphoreType.DMA((2, hops, 3)),
            pltpu.SemaphoreType.DMA((2, hops, 3)),
            pltpu.SemaphoreType.DMA((max(subs - 1, 1), chips, 3)),
            pltpu.SemaphoreType.DMA((max(subs - 1, 1), chips, 3)),
            pltpu.SemaphoreType.DMA((2,)),
        ],
        compiler_params=pltpu.CompilerParams(collective_id=0, has_side_effects=True),
        name="ring_gather",
    )(block, notes)


def ring_scatter(part, chips, subs, fold):
    hops = max(chips // 2, 1)
    rows, width = part.shape[2:]
    vmem = pl.BlockSpec(memory_space=pltpu.VMEM)
    return pl.pallas_call(
        functools.partial(scatter_kernel, chips, subs, fold),
        out_shape=jax.ShapeDtypeStruct((rows, width), part.dtype),
        in_specs=[vmem],
        out_specs=vmem,
        scratch_shapes=[
            pltpu.VMEM((max(subs - 1, 1), chips, rows, width), part.dtype),
            pltpu.VMEM((2, hops, rows, width), part.dtype),
            pltpu.VMEM((2, hops, rows, width), part.dtype),
            pltpu.SemaphoreType.DMA((2, hops, 2)),
            pltpu.SemaphoreType.DMA((2, hops, 2)),
            pltpu.SemaphoreType.DMA((max(subs - 1, 1), chips)),
            pltpu.SemaphoreType.DMA((max(subs - 1, 1), chips)),
        ],
        compiler_params=pltpu.CompilerParams(collective_id=1, has_side_effects=True),
        name="ring_scatter",
    )(part)


def normalize(states, norm_gain):
    values = states.astype(jnp.float32)
    spread = jnp.mean(values * values, axis=-1, keepdims=True)
    return (values * lax.rsqrt(spread + 1e-06) * norm_gain).astype(jnp.bfloat16)


def on_device(
    fold,
    hidden_state,
    norm_gain,
    router_weight,
    expert_ids,
    live_counts,
    routed_gate_up,
    routed_down,
    shared_weights,
):
    tok_rows, width = hidden_state.shape
    choose = expert_ids.shape[1]
    local_experts = routed_gate_up.shape[0]
    hidden_units = routed_down.shape[1]
    chips = lax.axis_size("expert")
    subs = lax.axis_size("sub")
    devices = chips * subs
    all_experts = local_experts * devices
    all_tokens = tok_rows * devices
    capacity = (tok_rows * choose * 4 + 3 * all_experts - 1) // (3 * all_experts)
    sub = lax.axis_index("sub")
    chip = lax.axis_index("expert")
    me = chip * subs + sub

    normed = normalize(hidden_state, norm_gain)
    probs = jax.nn.sigmoid(jnp.dot(normed, router_weight, preferred_element_type=jnp.float32))
    live = (jnp.arange(tok_rows, dtype=jnp.int32) < live_counts[0]).astype(jnp.float32)
    columns = jnp.arange(all_experts, dtype=jnp.int32)
    hot = jnp.sum((expert_ids[:, :, None] == columns[None, None, :]).astype(jnp.float32), axis=1)
    picked = hot * probs
    weights = live[:, None] * picked / jnp.sum(picked, axis=-1, keepdims=True)
    gate = probs * live[:, None]
    high = gate.astype(jnp.bfloat16)
    low = (gate - high.astype(jnp.float32)).astype(jnp.bfloat16)
    notes = jnp.concatenate(
        [weights.astype(jnp.bfloat16), (hot * live[:, None]).astype(jnp.bfloat16), high, low], axis=-1
    )
    spare = -notes.shape[1] % 128
    notes = jnp.pad(notes, ((0, 0), (0, spare)))
    everyone, notes = ring_gather(normed, notes, chips, subs, fold)

    notes = notes.astype(jnp.float32)
    place = ring_place(chip, chips, fold)
    origin = (
        ring_chip((place + jnp.arange(chips)[None, :]) % chips, chips, fold) * subs
        + (sub + jnp.arange(subs)[:, None]) % subs
    ).reshape(devices)
    sums = jnp.sum(notes.reshape(devices, tok_rows, -1), axis=1)
    at = origin[None, :] == jnp.arange(devices)[:, None]
    sums = jnp.sum(jnp.where(at[:, :, None], sums[None], 0.0), axis=1)
    sums = jnp.sum(sums, axis=0)
    load = sums[all_experts : 2 * all_experts]
    mass = sums[2 * all_experts : 3 * all_experts] + sums[3 * all_experts : 4 * all_experts]
    penalty = all_experts * jnp.sum(load * mass) / (choose * float(all_tokens) * float(all_tokens))

    everyone = everyone.reshape(all_tokens, width)
    notes = notes.reshape(all_tokens, -1)
    lanes = jnp.arange(notes.shape[1])
    owner = jnp.arange(all_tokens, dtype=jnp.int32) // tok_rows
    cells = jnp.arange(devices * capacity, dtype=jnp.int32)
    before = (jnp.arange(tok_rows)[:, None] < jnp.arange(tok_rows)[None, :]).astype(jnp.float32)
    mixed = None
    for item in range(local_experts):
        column = me * local_experts + item
        weight = jnp.sum(jnp.where(lanes[None, :] == column, notes, 0.0), axis=1)
        chosen = jnp.sum(jnp.where(lanes[None, :] == all_experts + column, notes, 0.0), axis=1)
        rank = jnp.dot(chosen.reshape(devices, tok_rows), before).reshape(all_tokens)
        spot = jnp.where(chosen > 0, rank.astype(jnp.int32) + owner * capacity, -1)
        match = spot[:, None] == cells[None, :]
        table = match.astype(jnp.bfloat16)
        mixing = jnp.where(match, weight[:, None], 0.0).astype(jnp.bfloat16)
        table, mixing = lax.optimization_barrier((table, mixing))
        rows = lax.dot_general(
            table, everyone, (((0,), (0,)), ((), ())), preferred_element_type=jnp.float32
        ).astype(jnp.bfloat16)
        inner = jnp.dot(rows, routed_gate_up[item], preferred_element_type=jnp.float32)
        active = (jax.nn.silu(inner[:, :hidden_units]) * inner[:, hidden_units:]).astype(
            jnp.bfloat16
        )
        results = jnp.dot(active, routed_down[item], preferred_element_type=jnp.float32).astype(
            jnp.bfloat16
        )
        part = jnp.dot(mixing, results, preferred_element_type=jnp.float32)
        mixed = part if mixed is None else mixed + part

    piece = everyone[: chips * tok_rows]
    gate_part = jnp.dot(piece, shared_weights[0], preferred_element_type=jnp.float32)
    up_part = jnp.dot(piece, shared_weights[1], preferred_element_type=jnp.float32)
    shared_active = (jax.nn.silu(gate_part) * up_part).astype(jnp.bfloat16)
    partials = lax.dot_general(
        shared_active,
        shared_weights[2],
        (((1,), (1,)), ((), ())),
        preferred_element_type=jnp.float32,
    )
    near = (mixed[: chips * tok_rows] + partials).astype(jnp.bfloat16)
    far = mixed[chips * tok_rows :].astype(jnp.bfloat16)
    total = jnp.concatenate([near, far], axis=0).reshape(subs, chips, tok_rows, width)
    return (ring_scatter(total, chips, subs, fold), penalty.reshape(1))


def fold_of(mesh):
    chips = mesh.shape["expert"]
    try:
        spots = [tuple(d.coords) for d in mesh.devices[0, :, 0].flat]
    except (AttributeError, TypeError, ValueError):
        spots = []
    if chips % 2 or chips < 4:
        return 1
    if len(spots) == chips:
        apart = sum(abs(a - b) for a, b in zip(spots[0], spots[2]))
        return 2 if apart == 1 else 1
    return 1


def solution(mesh):
    placed = (
        P(("groups", "expert", "sub"), None),
        P(),
        P(),
        P(("groups", "expert", "sub"), None),
        P(("groups", "expert", "sub")),
        P(("expert", "sub"), None, None),
        P(("expert", "sub"), None, None),
        P(None, None, "expert"),
    )
    return jax.shard_map(
        functools.partial(on_device, fold_of(mesh)),
        mesh=mesh,
        in_specs=placed,
        out_specs=(P(("groups", "expert", "sub"), None), P("groups")),
        check_vma=False,
    )
```

time: 186 us -> 125 us (0.67)
  waiting for transfers between devices: 96.1 us -> 0 us
  Pallas kernels: 0 us -> 63.1 us
  blocking collectives: 25.2 us -> 0 us
  between operations: 16.6 us -> 3.2 us
  other arithmetic: 4.37 us -> 9.99 us
  local copies, waits for them, and re-layouts: 2.62 us -> 6.67 us
    reduce_scatter x1 -> x0, waiting for transfers between devices: 70.1 us -> none  [on_device(): mixed = lax.psum_scatter(total, BOTH, scatter_dimension=0, tiled=True)]
    pallas_call x0 -> x2, Pallas kernels: none -> 63.1 us  [the longest x1 32.3 us: ring_gather(): pl.pallas_call(functools.partial(gather_kernel, chips, subs, fold), out_s...]
    all_gather x1 -> x0, waiting for transfers between devices: 26 us -> none  [on_device(): everyone = lax.all_gather(normed, BOTH, axis=0, tiled=True)]
    all_gather x1 -> x0, blocking collectives: 25.2 us -> none  [on_device(): notes = lax.all_gather(notes, BOTH, axis=0, tiled=True)]
    dot_general x3 -> x1, matrix products: 10.6 us -> 0.13 us  [on_device(): jnp.dot(chosen.reshape(devices, tok_rows), before).reshape(all_tokens)]
    dot_general x1, matrix products: 4.48 us -> 13.4 us  [on_device(): part = jnp.dot(mixing, results, preferred_element_type=jnp.float32)]
    slice x0 -> x2, local copies, waits for them, and re-layouts: none -> 4.37 us  [the longest x1 2.64 us: on_device(): far = mixed[chips * tok_rows:].astype(jnp.bfloat16)]
    concatenate x0 -> x2, other arithmetic: none -> 3.2 us  [the longest x1 2.51 us: on_device(): jnp.concatenate([near, far], axis=0).reshape(subs, chips, tok_rows, width)]
  transfers between devices with their start and end apart: 2 -> 0, of which waited for: 2 -> 0; matrix products, arithmetic and copies ran while one was open for 2% -> 0% of each run, Pallas kernels for 0% -> 0%
where the time goes in v2:
time: 125 us; the launch traced here: 124 us
  Pallas kernels  63.1 us (50%)
  matrix products  41.1 us (33%)
  other arithmetic  9.99 us (8%)
  local copies, waits for them, and re-layouts  6.67 us (5%)
  between operations  3.2 us (3%)
    pallas_call x1, Pallas kernels, ring_gather(): pl.pallas_call(functools.partial(gather_kernel, chips, subs, fold), out_s...  32.3 us
    pallas_call x1, Pallas kernels, ring_scatter(): pl.pallas_call(functools.partial(scatter_kernel, chips, subs, fold), out_...  30.8 us
    dot_general x1, matrix products, on_device(): jnp.dot(rows, routed_gate_up[item], preferred_element_type=jnp.float32)  17.3 us
    dot_general x1, matrix products, on_device(): part = jnp.dot(mixing, results, preferred_element_type=jnp.float32)  13.4 us
    dot_general x1, matrix products, on_device(): lax.dot_general(shared_active, shared_weights[2], (((1,), (1,)), ((), ())...  6.89 us
    dot_general x1, matrix products, on_device(): jnp.dot(piece, shared_weights[0], preferred_element_type=jnp.float32)  3.16 us
    slice x1, local copies, waits for them, and re-layouts, on_device(): far = mixed[chips * tok_rows:].astype(jnp.bfloat16)  2.64 us
    concatenate x1, other arithmetic, on_device(): jnp.concatenate([near, far], axis=0).reshape(subs, chips, tok_rows, width)  2.51 us

profile of v2, /device:TPU:0, one launch (start us, length us, event | category | flops | bytes accessed | tf_op | source)
XLA Modules:
  0.0 124.1 jit_solution(11094900018595193247)
XLA Ops:
  0.6 0.0 copy-start
  1.4 0.1 broadcast_add_fusion
  1.4 0.1 add.160
  1.5 1.1 fusion.36
  2.7 0.7 convert_reduce_fusion.1
  3.4 0.1 copy.16
  3.5 1.1 fusion.38.block_ref
  4.5 0.0 copy-done
  4.6 0.0 copy-start.2
  4.6 0.3 multiply_reduce_fusion
  4.9 0.1 divide_convert_fusion
  5.0 0.7 fusion.53.notes_ref
  5.7 0.0 copy-done.2
  5.7 32.3 %ring_gather.1 = (bf16[2,8,64,2048]{3,2,1,0:T(8,128)(2,1)}, bf16[2,8,64,128]{3,2,1,0:T(8,128)(2,1)}) custom-call(bf16[64,2048]{1,0:T(8,128)(2,1)} %copy-done.2, bf16[64,128]{1,0:T(8,128)(2,1)} %fusion.53.notes_ref), custom_call_target="tpu_custom_call" | custom-call | tf_op jit(solution)/shard_map/ring_gather/pallas_call | solution.py:228
  38.0 1.3 %convert_reduce_fusion = (f32[2,8,128]{2,1,0:T(8,128)S(1)}, bf16[2,8,64]{2,1,0:T(8,128)(2,1)S(1)}, f32[2,8,64]{2,1,0:T(8,128)S(1)}) fusion(bf16[2,8,64,128]{3,2,1,0:T(8,128)(2,1)} %get-tuple-element.6, pred[128]{0:T(512)(128)(4,1)S(1)} %get-tuple-element.19, pred[128]{0:T(512)(128)(4,1)S(1)} %get-tuple-element.20), kind=kLoop, calls=%fused_computation.31 | loop fusion | flops 782336 | bytes 276736 | tf_op jit(solution)/shard_map/reduce_sum | solution.py:325
  39.3 0.1 select_reduce_fusion
  39.4 0.7 multiply_reduce_fusion.1
  40.8 0.1 broadcast_in_dim.79
  40.8 0.1 gt.15
  40.9 0.1 convolution_convert_fusion.1
  41.1 0.1 convert_element_type.80
  41.1 0.3 select_convert_fusion
  41.5 1.2 fusion.9
  42.7 1.7 %slice.40 = bf16[1,8,64,2048]{3,2,1,0:T(8,128)(2,1)S(1)} slice(bf16[2,8,64,2048]{3,2,1,0:T(8,128)(2,1)} %get-tuple-element.9), slice={[0:1], [0:8], [0:64], [0:2048]} | slice | bytes 4194304 | tf_op jit(solution)/shard_map/slice | solution.py:363
  44.4 3.2 %fusion.14 = f32[512,352]{0,1:T(8,128)} fusion(bf16[512,2048]{1,0:T(8,128)(2,1)S(1)} %bitcast.52, bf16[3,2048,352]{1,2,0:T(8,128)(2,1)} %param.15), kind=kOutput, calls=%fused_computation.18 | convolution fusion | flops 738197504 | bytes 4259840 | tf_op jit(solution)/shard_map/dot_general | solution.py:364
  47.6 17.3 %fusion = f32[512,2816]{1,0:T(8,128)} fusion(bf16[1,2048,2816]{2,1,0:T(8,128)(2,1)} %param.13, bf16[1024,512]{1,0:T(8,128)(2,1)} %fusion.9, bf16[1024,2048]{1,0:T(8,128)(2,1)} %bitcast.54), kind=kOutput, calls=%fused_computation | convolution fusion | flops 8054112256 | bytes 22544384 | tf_op jit(solution)/shard_map/dot_general | solution.py:353
  64.9 13.4 %fusion.43 = f32[1024,2048]{1,0:T(8,128)} fusion(bf16[1024,512]{1,0:T(8,128)(2,1)S(1)} %select_convert_fusion, bf16[1,1408,2048]{2,1,0:T(8,128)(2,1)} %param.14, f32[512,2816]{1,0:T(8,128)} %fusion), kind=kOutput, calls=%fused_computation.46 | convolution fusion | flops 5105647616 | bytes 20971520 | tf_op jit(solution)/shard_map/dot_general | solution.py:360
  78.2 6.9 %fusion.4 = bf16[512,2048]{1,0:T(8,128)(2,1)} fusion(f32[1024,2048]{1,0:T(8,128)} %fusion.43, bf16[3,2048,352]{1,2,0:T(8,128)(2,1)} %param.15, bf16[512,2048]{1,0:T(8,128)(2,1)S(1)} %bitcast.53, f32[512,352]{0,1:T(8,128)} %fusion.14), kind=kOutput, calls=%fused_computation.6 | convolution fusion | flops 1479573504 | bytes 11993088 | tf_op jit(solution)/shard_map/dot_general | solution.py:367
  85.1 0.0 copy-start.1
  85.1 2.6 %slice.88 = bf16[512,2048]{1,0:T(8,128)(2,1)S(1)} slice(f32[1024,2048]{1,0:T(8,128)} %fusion.43), slice={[512:1024], [0:2048]} | slice | bytes 4194304 | tf_op jit(solution)/shard_map/slice | solution.py:374
  87.8 0.2 copy-done.1
  88.0 2.5 %pad_maximum_fusion = bf16[1024,2048]{1,0:T(8,128)(2,1)} fusion(bf16[512,2048]{1,0:T(8,128)(2,1)S(1)} %slice.88, bf16[512,2048]{1,0:T(8,128)(2,1)S(1)} %copy-done.1), kind=kLoop, calls=%fused_computation.7 | loop fusion | flops 8388608 | bytes 8388608 | tf_op jit(solution)/shard_map/concatenate | solution.py:375
  90.5 30.8 %ring_scatter.1 = bf16[64,2048]{1,0:T(8,128)(2,1)} custom-call(bf16[2,8,64,2048]{3,2,1,0:T(8,128)(2,1)} %bitcast.51), custom_call_target="tpu_custom_call" | custom-call | tf_op jit(solution)/shard_map/ring_scatter/pallas_call | solution.py:252
  121.3 1.7 %copy.24 = bf16[64,2048]{1,0:T(8,128)(2,1)} copy(bf16[64,2048]{1,0:T(8,128)(2,1)} %ring_scatter.1) | data formatting | bytes 524288
  (8 shorter events, 0.1 us)
Async XLA Ops:
  0.6 3.9 %copy-start = (bf16[2048,16]{0,1:T(8,128)(2,1)S(1)}, bf16[2048,16]{0,1:T(8,128)(2,1)}, u32[]{:S(2)}) copy-start(bf16[2048,16]{0,1:T(8,128)(2,1)} %param.10) | copy-start | bytes 196612
  4.6 1.1 copy-start.2
  85.1 2.9 %copy-start.1 = (bf16[512,2048]{1,0:T(8,128)(2,1)S(1)}, bf16[512,2048]{1,0:T(8,128)(2,1)}, u32[]{:S(2)}) copy-start(bf16[512,2048]{1,0:T(8,128)(2,1)} %fusion.4) | copy-start | bytes 6291460

commit v3 on v2

--- a/solution.py
+++ b/solution.py
@@ -137,9 +137,10 @@
 
 
 def scatter_kernel(
-    chips, subs, fold, part_ref, out_ref, from_peer, going, coming,
-    ring_send, ring_recv, peer_send, peer_recv,
+    chips, subs, fold, *refs,
 ):
+    parts = refs[:subs]
+    out_ref, from_peer, going, coming, ring_send, ring_recv, peer_send, peer_recv = refs[subs:]
     along, peers = neighbours(chips, subs, fold)
     rows = out_ref.shape[0]
     half = rows // 2
@@ -148,7 +149,7 @@
     def peer_copy(i, k):
         k = k % chips
         return pltpu.make_async_remote_copy(
-            src_ref=part_ref.at[i, k],
+            src_ref=parts[i].at[k],
             dst_ref=from_peer.at[i - 1, k],
             send_sem=peer_send.at[i - 1, k],
             recv_sem=peer_recv.at[i - 1, k],
@@ -169,7 +170,7 @@
 
     def local_sum(k, j):
         span = pl.ds(j * half, half)
-        value = part_ref[0, k % chips, span, :].astype(jnp.float32)
+        value = parts[0][k % chips, span, :].astype(jnp.float32)
         for i in range(1, subs):
             value = value + from_peer[i - 1, k % chips, span, :].astype(jnp.float32)
         return value
@@ -245,19 +246,19 @@
     )(block, notes)
 
 
-def ring_scatter(part, chips, subs, fold):
+def ring_scatter(parts, chips, subs, fold):
     hops = max(chips // 2, 1)
-    rows, width = part.shape[2:]
+    rows, width = parts[0].shape[1:]
     vmem = pl.BlockSpec(memory_space=pltpu.VMEM)
     return pl.pallas_call(
         functools.partial(scatter_kernel, chips, subs, fold),
-        out_shape=jax.ShapeDtypeStruct((rows, width), part.dtype),
-        in_specs=[vmem],
+        out_shape=jax.ShapeDtypeStruct((rows, width), parts[0].dtype),
+        in_specs=[vmem] * subs,
         out_specs=vmem,
         scratch_shapes=[
-            pltpu.VMEM((max(subs - 1, 1), chips, rows, width), part.dtype),
-            pltpu.VMEM((2, hops, rows, width), part.dtype),
-            pltpu.VMEM((2, hops, rows, width), part.dtype),
+            pltpu.VMEM((max(subs - 1, 1), chips, rows, width), parts[0].dtype),
+            pltpu.VMEM((2, hops, rows, width), parts[0].dtype),
+            pltpu.VMEM((2, hops, rows, width), parts[0].dtype),
             pltpu.SemaphoreType.DMA((2, hops, 2)),
             pltpu.SemaphoreType.DMA((2, hops, 2)),
             pltpu.SemaphoreType.DMA((max(subs - 1, 1), chips)),
@@ -265,7 +266,7 @@
         ],
         compiler_params=pltpu.CompilerParams(collective_id=1, has_side_effects=True),
         name="ring_scatter",
-    )(part)
+    )(*parts)
 
 
 def normalize(states, norm_gain):
@@ -330,50 +331,57 @@
     mass = sums[2 * all_experts : 3 * all_experts] + sums[3 * all_experts : 4 * all_experts]
     penalty = all_experts * jnp.sum(load * mass) / (choose * float(all_tokens) * float(all_tokens))
 
-    everyone = everyone.reshape(all_tokens, width)
-    notes = notes.reshape(all_tokens, -1)
-    lanes = jnp.arange(notes.shape[1])
-    owner = jnp.arange(all_tokens, dtype=jnp.int32) // tok_rows
-    cells = jnp.arange(devices * capacity, dtype=jnp.int32)
+    span = chips * tok_rows
+    slots = chips * capacity
+    everyone = everyone.reshape(subs, span, width)
+    notes = notes.reshape(subs, span, -1)
+    lanes = jnp.arange(notes.shape[2])
+    owner = jnp.arange(span, dtype=jnp.int32) // tok_rows
+    cells = jnp.arange(slots, dtype=jnp.int32)
     before = (jnp.arange(tok_rows)[:, None] < jnp.arange(tok_rows)[None, :]).astype(jnp.float32)
-    mixed = None
+    mixed = [0.0] * subs
     for item in range(local_experts):
         column = me * local_experts + item
-        weight = jnp.sum(jnp.where(lanes[None, :] == column, notes, 0.0), axis=1)
-        chosen = jnp.sum(jnp.where(lanes[None, :] == all_experts + column, notes, 0.0), axis=1)
-        rank = jnp.dot(chosen.reshape(devices, tok_rows), before).reshape(all_tokens)
+        weight = jnp.sum(jnp.where(lanes == column, notes, 0.0), axis=2)
+        chosen = jnp.sum(jnp.where(lanes == all_experts + column, notes, 0.0), axis=2)
+        rank = jnp.dot(chosen.reshape(devices, tok_rows), before).reshape(subs, span)
         spot = jnp.where(chosen > 0, rank.astype(jnp.int32) + owner * capacity, -1)
-        match = spot[:, None] == cells[None, :]
+        match = spot[:, :, None] == cells
         table = match.astype(jnp.bfloat16)
-        mixing = jnp.where(match, weight[:, None], 0.0).astype(jnp.bfloat16)
+        mixing = jnp.where(match, weight[:, :, None], 0.0).astype(jnp.bfloat16)
         table, mixing = lax.optimization_barrier((table, mixing))
         rows = lax.dot_general(
-            table, everyone, (((0,), (0,)), ((), ())), preferred_element_type=jnp.float32
-        ).astype(jnp.bfloat16)
+            table, everyone, (((1,), (1,)), ((0,), (0,))), preferred_element_type=jnp.float32
+        ).astype(jnp.bfloat16).reshape(subs * slots, width)
+        rows = lax.optimization_barrier(rows)
         inner = jnp.dot(rows, routed_gate_up[item], preferred_element_type=jnp.float32)
         active = (jax.nn.silu(inner[:, :hidden_units]) * inner[:, hidden_units:]).astype(
             jnp.bfloat16
         )
+        active = lax.optimization_barrier(active)
         results = jnp.dot(active, routed_down[item], preferred_element_type=jnp.float32).astype(
             jnp.bfloat16
         )
-        part = jnp.dot(mixing, results, preferred_element_type=jnp.float32)
-        mixed = part if mixed is None else mixed + part
-
-    piece = everyone[: chips * tok_rows]
+        results = lax.optimization_barrier(results)
+        for r in range(subs):
+            mixed[r] = mixed[r] + jnp.dot(
+                mixing[r], results[r * slots : (r + 1) * slots], preferred_element_type=jnp.float32
+            )
+
+    piece = everyone[0]
     gate_part = jnp.dot(piece, shared_weights[0], preferred_element_type=jnp.float32)
     up_part = jnp.dot(piece, shared_weights[1], preferred_element_type=jnp.float32)
     shared_active = (jax.nn.silu(gate_part) * up_part).astype(jnp.bfloat16)
+    shared_active = lax.optimization_barrier(shared_active)
     partials = lax.dot_general(
         shared_active,
         shared_weights[2],
         (((1,), (1,)), ((), ())),
         preferred_element_type=jnp.float32,
     )
-    near = (mixed[: chips * tok_rows] + partials).astype(jnp.bfloat16)
-    far = mixed[chips * tok_rows :].astype(jnp.bfloat16)
-    total = jnp.concatenate([near, far], axis=0).reshape(subs, chips, tok_rows, width)
-    return (ring_scatter(total, chips, subs, fold), penalty.reshape(1))
+    mixed[0] = mixed[0] + partials
+    parts = [part.astype(jnp.bfloat16).reshape(chips, tok_rows, width) for part in mixed]
+    return (ring_scatter(parts, chips, subs, fold), penalty.reshape(1))
 
 
 def fold_of(mesh):

time: 125 us -> 100 us (0.80)
  matrix products: 41.1 us -> 21.5 us
  other arithmetic: 9.99 us -> 7.06 us
  local copies, waits for them, and re-layouts: 6.67 us -> 4.79 us
    dot_general x1, matrix products: 17.3 us -> 6.2 us  [on_device(): jnp.dot(rows, routed_gate_up[item], preferred_element_type=jnp.float32)]
    dot_general x1, matrix products: 6.89 us -> 2.73 us  [on_device(): lax.dot_general(shared_active, shared_weights[2], (((1,), (1,)), ((), ())...]
    slice x2 -> x1, local copies, waits for them, and re-layouts: 4.37 us -> 0.24 us  [on_device(): piece = everyone[0]]
    concatenate x1 -> x0, other arithmetic: 2.51 us -> none  [on_device(): jnp.concatenate([near, far], axis=0).reshape(subs, chips, tok_rows, width)]
    unnamed x7 -> x19, local copies, waits for them, and re-layouts: 1.88 us -> 4.14 us
    dot_general x1, matrix products: 3.16 us -> 0.94 us  [on_device(): jnp.dot(piece, shared_weights[0], preferred_element_type=jnp.float32)]
    dot_general x2 -> x6, matrix products: 13.5 us -> 11.3 us  [the longest x1 3.81 us: on_device(): jnp.dot(active, routed_down[item], preferred_element_type=jnp.float32)]
where the time goes in v3:
time: 100 us; the launch traced here: 99.8 us
  Pallas kernels  63.1 us (63%)
  matrix products  21.5 us (22%)
  other arithmetic  7.06 us (7%)
  local copies, waits for them, and re-layouts  4.79 us (5%)
  between operations  3.34 us (3%)
    pallas_call x1, Pallas kernels, ring_gather(): pl.pallas_call(functools.partial(gather_kernel, chips, subs, fold), out_s...  32.3 us
    pallas_call x1, Pallas kernels, ring_scatter(): pl.pallas_call(functools.partial(scatter_kernel, chips, subs, fold), out_...  30.8 us
    dot_general x1, matrix products, on_device(): jnp.dot(rows, routed_gate_up[item], preferred_element_type=jnp.float32)  6.2 us
    unnamed x19, local copies, waits for them, and re-layouts  4.14 us
    dot_general x1, matrix products, on_device(): jnp.dot(active, routed_down[item], preferred_element_type=jnp.float32)  3.81 us
    dot_general x1, matrix products, on_device(): lax.dot_general(table, everyone, (((1,), (1,)), ((0,), (0,))), preferred_...  3.6 us
    dot_general x2, matrix products, on_device(): jnp.dot(mixing[r], results[r * slots:(r + 1) * slots], preferred_element_...  2.79 us
    dot_general x1, matrix products, on_device(): lax.dot_general(shared_active, shared_weights[2], (((1,), (1,)), ((), ())...  2.73 us

profile of v3, /device:TPU:0, one launch (start us, length us, event | category | flops | bytes accessed | tf_op | source)
XLA Modules:
  0.0 99.8 jit_solution(1035824712889063030)
XLA Ops:
  0.6 0.0 copy-start
  1.4 0.1 broadcast_add_fusion
  1.4 0.1 add.166
  1.5 1.1 %fusion.29 = f32[64]{0:T(128)S(1)} fusion(bf16[64,2048]{1,0:T(8,128)(2,1)} %param.8), kind=kLoop, calls=%fused_computation.36 | loop fusion | flops 393152 | bytes 262400 | tf_op jit(solution)/shard_map/reduce_sum | solution.py:274
  2.7 0.7 convert_reduce_fusion.1
  3.4 0.1 copy.16
  3.5 1.1 %fusion.31.block_ref = bf16[64,2048]{1,0:T(8,128)(2,1)S(1)} fusion(bf16[64,2048]{1,0:T(8,128)(2,1)} %param.8, f32[2048]{0:T(1024)} %param.9, f32[64]{0:T(128)S(1)} %add_rsqrt_fusion), kind=kLoop, calls=%fused_computation.38 | loop fusion | flops 524288 | bytes 532736 | tf_op jit(solution)/shard_map/convert_element_type | solution.py:275
  4.6 0.0 copy-done
  4.6 0.0 copy-start.2
  4.6 0.3 multiply_reduce_fusion
  4.9 0.1 divide_convert_fusion
  5.0 0.7 fusion.44.notes_ref
  5.7 0.0 copy-done.2
  5.7 32.3 %ring_gather.1 = (bf16[2,8,64,2048]{3,2,1,0:T(8,128)(2,1)}, bf16[2,8,64,128]{3,2,1,0:T(8,128)(2,1)}) custom-call(bf16[64,2048]{1,0:T(8,128)(2,1)} %copy-done.2, bf16[64,128]{1,0:T(8,128)(2,1)} %fusion.44.notes_ref), custom_call_target="tpu_custom_call" | custom-call | tf_op jit(solution)/shard_map/ring_gather/pallas_call | solution.py:229
  38.0 1.3 %convert_reduce_fusion = (f32[2,8,128]{2,1,0:T(8,128)S(1)}, bf16[2,8,64]{2,1,0:T(8,128)(2,1)S(1)}, f32[2,8,64]{2,1,0:T(8,128)S(1)}) fusion(bf16[2,8,64,128]{3,2,1,0:T(8,128)(2,1)} %get-tuple-element.6, pred[128]{0:T(512)(128)(4,1)S(1)} %get-tuple-element.19, pred[128]{0:T(512)(128)(4,1)S(1)} %get-tuple-element.20), kind=kLoop, calls=%fused_computation.31 | loop fusion | flops 782336 | bytes 276736 | tf_op jit(solution)/shard_map/reduce_sum | solution.py:326
  39.3 0.1 select_reduce_fusion
  39.4 0.7 multiply_reduce_fusion.1
  40.8 0.1 broadcast_in_dim.75
  40.9 0.1 convolution_convert_fusion.2
  41.0 0.1 convert_element_type.82
  41.1 0.1 gt.15
  41.2 0.2 select_convert_fusion
  41.3 0.1 fusion.28
  41.5 0.0 copy-start.1
  41.5 0.0 copy-start.3
  41.5 3.6 %convolution_convert_fusion.1 = bf16[2,256,2048]{2,1,0:T(8,128)(2,1)S(1)} fusion(bf16[2,512,256]{1,2,0:T(8,128)(2,1)S(1)} %fusion.28, bf16[2,512,2048]{2,1,0:T(8,128)(2,1)} %bitcast.57), kind=kOutput, calls=%fused_computation.6 | convolution fusion | flops 1074790400 | bytes 6815744 | tf_op jit(solution)/shard_map/dot_general | solution.py:353
  45.1 0.0 copy-done.1
  45.1 0.0 slice-start
  45.1 0.2 slice.44
  45.4 0.9 copy-done.3
  46.2 0.0 slice-start.1
  46.2 0.9 fusion.11
  47.2 0.0 slice-start.2
  47.2 0.0 slice-start.3
  47.2 1.0 fusion.19
  48.2 0.0 slice-done
  48.2 0.6 slice-done.1
  48.8 1.0 slice-done.2
  49.8 6.2 %fusion = f32[512,2816]{1,0:T(8,128)S(1)} fusion(bf16[512,2048]{1,0:T(8,128)(2,1)S(1)} %bitcast.60, bf16[1,2048,2816]{2,1,0:T(8,128)(2,1)S(1)} %bitcast.65), kind=kOutput, calls=%fused_computation | convolution fusion | flops 5905580032 | bytes 19398656 | tf_op jit(solution)/shard_map/dot_general | solution.py:357
  56.0 0.9 fusion.7
  56.8 0.0 slice-done.3
  56.8 0.0 slice-done.4
  56.8 3.8 %fusion.4 = bf16[512,2048]{1,0:T(8,128)(2,1)S(1)} fusion(bf16[512,1408]{1,0:T(8,128)(2,1)S(1)} %fusion.7, bf16[1,1408,2048]{2,1,0:T(8,128)(2,1)S(1)} %bitcast.67), kind=kOutput, calls=%fused_computation.7 | convolution fusion | flops 2953838592 | bytes 9306112 | tf_op jit(solution)/shard_map/dot_general | solution.py:362
  60.7 2.0 %convolution_convert_fusion = bf16[512,2048]{1,0:T(8,128)(2,1)} fusion(bf16[512,2048]{1,0:T(8,128)(2,1)S(1)} %fusion.4, bf16[2,512,256]{1,2,0:T(8,128)(2,1)S(1)} %select_convert_fusion), kind=kOutput, calls=%fused_computation.5 | convolution fusion | flops 537919488 | bytes 3407872 | tf_op jit(solution)/shard_map/dot_general | solution.py:367
  62.7 0.7 fusion.26
  63.4 2.7 %add_convert_fusion = bf16[512,2048]{1,0:T(8,128)(2,1)} fusion(f32[512,2048]{1,0:T(8,128)S(1)} %fusion.26, bf16[512,352]{0,1:T(8,128)(2,1)S(1)} %fusion.19, bf16[3,2048,352]{1,2,0:T(8,128)(2,1)S(1)} %copy-done.3), kind=kOutput, calls=%fused_computation.4 | convolution fusion | flops 740294656 | bytes 8093696 | tf_op jit(solution)/shard_map/dot_general | solution.py:376
  66.2 30.8 %ring_scatter.1 = bf16[64,2048]{1,0:T(8,128)(2,1)} custom-call(bf16[8,64,2048]{2,1,0:T(8,128)(2,1)} %bitcast.59, bf16[8,64,2048]{2,1,0:T(8,128)(2,1)} %bitcast.58), custom_call_target="tpu_custom_call" | custom-call | tf_op jit(solution)/shard_map/ring_scatter/pallas_call | solution.py:253
  97.0 1.7 %copy.24 = bf16[64,2048]{1,0:T(8,128)(2,1)} copy(bf16[64,2048]{1,0:T(8,128)(2,1)} %ring_scatter.1) | data formatting | bytes 524288
  (12 shorter events, 0.1 us)
Async XLA Ops:
  0.6 3.9 %copy-start = (bf16[2048,16]{0,1:T(8,128)(2,1)S(1)}, bf16[2048,16]{0,1:T(8,128)(2,1)}, u32[]{:S(2)}) copy-start(bf16[2048,16]{0,1:T(8,128)(2,1)} %param.10) | copy-start | bytes 196612
  4.6 1.1 %copy-start.2 = (bf16[64,2048]{1,0:T(8,128)(2,1)}, bf16[64,2048]{1,0:T(8,128)(2,1)S(1)}, u32[]{:S(2)}) copy-start(bf16[64,2048]{1,0:T(8,128)(2,1)S(1)} %fusion.31.block_ref) | copy-start | bytes 786436
  41.5 3.6 %copy-start.1 = (bf16[2,8,64,2048]{3,2,1,0:T(8,128)(2,1)S(1)}, bf16[2,8,64,2048]{3,2,1,0:T(8,128)(2,1)}, u32[]{:S(2)}) copy-start(bf16[2,8,64,2048]{3,2,1,0:T(8,128)(2,1)} %get-tuple-element.9) | copy-start | bytes 12582916
  41.5 4.8 %copy-start.3 = (bf16[3,2048,352]{1,2,0:T(8,128)(2,1)S(1)}, bf16[3,2048,352]{1,2,0:T(8,128)(2,1)}, u32[]{:S(2)}) copy-start(bf16[3,2048,352]{1,2,0:T(8,128)(2,1)} %param.15) | copy-start | bytes 12976132
  45.1 3.1 %slice-start = ((s8[11534336]{0:T(1024)(128)(4,1)}), s8[4194304]{0:T(1024)(128)(4,1)S(1)}, s32[]{:S(2)}) async-start(s8[11534336]{0:T(1024)(128)(4,1)} %bitcast.64), calls=%async_computation | async-start | bytes 8388608
  46.2 2.6 %slice-start.1 = ((s8[11534336]{0:T(1024)(128)(4,1)}), s8[4194304]{0:T(1024)(128)(4,1)S(1)}, s32[]{:S(2)}) async-start(s8[11534336]{0:T(1024)(128)(4,1)} %bitcast.64), calls=%async_computation.1 | async-start | bytes 8388608
  47.2 2.6 %slice-start.2 = ((s8[11534336]{0:T(1024)(128)(4,1)}), s8[3145728]{0:T(1024)(128)(4,1)S(1)}, s32[]{:S(2)}) async-start(s8[11534336]{0:T(1024)(128)(4,1)} %bitcast.64), calls=%async_computation.2 | async-start | bytes 6291456
  47.2 9.6 %slice-start.3 = ((s8[5767168]{0:T(1024)(128)(4,1)}), s8[4194304]{0:T(1024)(128)(4,1)S(1)}, s32[]{:S(2)}) async-start(s8[5767168]{0:T(1024)(128)(4,1)} %bitcast.66), calls=%async_computation.3 | async-start | bytes 8388608
  49.8 7.1 %slice-start.4 = ((s8[5767168]{0:T(1024)(128)(4,1)}), s8[1572864]{0:T(1024)(128)(4,1)S(1)}, s32[]{:S(2)}) async-start(s8[5767168]{0:T(1024)(128)(4,1)} %bitcast.66), calls=%async_computation.4 | async-start | bytes 3145728
